TPU v7x, 512 devices: a whole 4x4x16 slice. The times are simulated.
512 devices in a mesh: phase: 8 (over y, core), wide: 64 (over x, z).
Axes of the slice: x: 4, y: 4, z: 16, core: 2. Of those that a mesh axis runs over, the one named last changes fastest.
Arguments:
- image: bfloat16 [16, 256, 16384], P(None, None, 'wide'), may hold values from -6 to 6
- conv_weight: bfloat16 [8, 256, 2304], P('phase'), may hold values from -0.09375 to 0.09375
- class_weight: bfloat16 [11, 256], replicated, may hold values from -0.375 to 0.375
- point_feats: float32 [16, 4, 16384], P('phase', None, 'wide'), may hold values from -6 to 6
- pixel_index: int32 [16, 16384], P('phase', 'wide'), may hold values from 0 to 16383
- pillar_index: int32 [16, 16384], P('phase', 'wide'), may hold values from 0 to 8191
- point_counts: int32 [16, 64], P('phase', 'wide'), may hold values from 64 to 256, as said below
- pillar_weight: float32 [64, 15], replicated, may hold values from -1.5 to 1.5
- bev_weight: bfloat16 [576, 384], replicated, may hold values from -0.25 to 0.25
- head_weight: bfloat16 [384, 20], replicated, may hold values from -0.3125 to 0.3125
Outputs:
- detections: float32 [16, 8192, 20], P('phase', 'wide')
- scores: float32 [16, 11, 16384], P('phase', None, 'wide')
Inputs may be any that keep to these rules, and one draw needn't show every extreme that they name: `point_counts`: in every frame some index of wide has all 256 slots live; slots at or past the count are padding.
All inputs are finite; a program needn't handle non-finite values.
Results may differ from a plain program's by a relative error of at most 0.01.
Values may be sent and summed in bfloat16 or wider, within the bound.
A program may use at most 64 MiB of HBM per device.

v0:
```python
import jax
import jax.numpy as jnp
from jax import lax
from jax.sharding import Mesh
from jax.sharding import PartitionSpec as P

PIL = 64
HEAD = 384
IMG_W = 64
BEV_W = 128
CELLS_DEV = 128
WIDE = ("wide_0", "wide_1")


def padded_2(value, sides, width):
    for axis, dim in sides:
        devices, length = (lax.axis_size(axis), value.shape[dim])
        up = [(i, (i + 1) % devices) for i in range(devices - 1)]
        down = [(j, i) for i, j in up]
        last = lax.slice_in_dim(value, length - width, length, axis=dim)
        first = lax.slice_in_dim(value, 0, width, axis=dim)
        before = lax.ppermute(last, axis, up)
        after = lax.ppermute(first, axis, down)
        value = jnp.concatenate([before, value, after], axis=dim)
    return value


def joined_along(parts, dim):
    dims = list(parts.shape[1:])
    dims[dim] *= parts.shape[0]
    return jnp.moveaxis(parts, 0, dim).reshape(dims)


def copy_for_each(value, axis):
    devices = lax.axis_size(axis)
    return lax.all_to_all(
        jnp.broadcast_to(value[None], (devices, *value.shape)), axis, 0, 0, tiled=True
    )


def gather_directly(value, axis, dim):
    return joined_along(copy_for_each(value, axis), dim)


def whole_of(value, axes, dim):
    filled = value
    for number in range(len(axes) - 1, -1, -1):
        filled = lax.all_gather(filled, axes[number], axis=dim, tiled=True)
    return filled


def image_layer(activation, weight):
    length = activation.shape[2]
    padded = padded_2(activation, ((WIDE, 2),), IMG_W)
    extended = jnp.pad(padded, ((0, 0), (0, 0), (1, 1)))
    column = jnp.arange(length, dtype=jnp.int32) % IMG_W
    sections = []
    for row_step in range(3):
        for col_step in range(3):
            offset = row_step * IMG_W + col_step
            section = lax.slice_in_dim(extended, offset, offset + length, axis=2)
            inside = (column + col_step - 1 >= 0) & (column + col_step - 1 < IMG_W)
            sections.append(jnp.where(inside[None, None, :], section, jnp.zeros_like(section)))
    stacked = jnp.concatenate(sections, axis=1)
    summed = jnp.einsum("ok,fkp->fop", weight, stacked, preferred_element_type=jnp.float32)
    return (activation.astype(jnp.float32) + jax.nn.relu(summed)).astype(jnp.bfloat16)


def bev_layer(grid, bev_weight, own_frames):
    padded = padded_2(grid, ((WIDE, 0),), BEV_W)
    extended = jnp.pad(padded, ((1, 1), (0, 0)))
    column = jnp.arange(CELLS_DEV, dtype=jnp.int32) % BEV_W
    sections = []
    for row_step in range(3):
        for col_step in range(3):
            offset = row_step * BEV_W + col_step
            section = lax.slice_in_dim(extended, offset, offset + CELLS_DEV, axis=0)
            inside = (column + col_step - 1 >= 0) & (column + col_step - 1 < BEV_W)
            sections.append(jnp.where(inside[:, None], section, jnp.zeros_like(section)))
    stacked = jnp.stack(sections, axis=1).reshape(CELLS_DEV, 9, own_frames, PIL)
    summed = jnp.einsum(
        "ctfj,tjo->fco",
        stacked,
        bev_weight.reshape(9, PIL, HEAD),
        preferred_element_type=jnp.float32,
    )
    return jax.nn.relu(summed).astype(jnp.bfloat16)


def local(
    image,
    conv_weight,
    class_weight,
    point_feats,
    pixel_index,
    pillar_index,
    point_counts,
    pillar_weight,
    bev_weight,
    head_weight,
):
    phase_now = lax.axis_index("phase")
    phases = lax.axis_size("phase")
    own_frames = point_feats.shape[0]
    weights = lax.all_gather(conv_weight, "phase", axis=0, tiled=True)
    start_maps = lax.dynamic_slice_in_dim(image, phase_now * own_frames, own_frames, 0)

    def layer_step(layer, activation):
        return image_layer(activation, lax.dynamic_index_in_dim(weights, layer, 0, keepdims=False))

    own_maps = lax.fori_loop(0, phases, layer_step, start_maps)
    scores = jnp.einsum("kc,fcp->fkp", class_weight, own_maps, preferred_element_type=jnp.float32)
    logits = scores.astype(jnp.bfloat16)
    section = gather_directly(logits, WIDE, 2)
    extent = section.shape[2]
    onehot = (pixel_index[:, None, :] == jnp.arange(extent, dtype=jnp.int32)[None, :, None]).astype(
        jnp.bfloat16
    )
    painted = jnp.einsum("fkn,fnp->fkp", section, onehot, preferred_element_type=jnp.float32)
    features = jnp.concatenate([point_feats, jax.nn.sigmoid(painted)], axis=1)
    hidden = jax.nn.relu(
        jnp.einsum("jd,fdp->fjp", pillar_weight, features, precision=lax.Precision.HIGHEST)
    )
    positions = jnp.arange(pixel_index.shape[1], dtype=jnp.int32)
    is_live = positions[None, :] < point_counts
    hidden = jnp.where(is_live[:, None, :], hidden, 0.0).astype(jnp.bfloat16)
    own_first = lax.axis_index(WIDE) * CELLS_DEV
    part_hidden = whole_of(hidden, ("wide_1", "wide_0"), 2)
    part_index = whole_of(pillar_index[:, None, :], ("wide_1", "wide_0"), 2)
    onehot = (
        part_index[:, 0, :, None] - own_first
        == jnp.arange(CELLS_DEV, dtype=jnp.int32)[None, None, :]
    ).astype(jnp.bfloat16)
    partial_sum = jnp.einsum(
        "fjp,fpc->cfj", part_hidden, onehot, preferred_element_type=jnp.float32
    )
    pooled = partial_sum.reshape(CELLS_DEV, own_frames * PIL)
    grid = pooled.astype(jnp.bfloat16)
    feature = bev_layer(grid, bev_weight, own_frames)
    detections = jnp.einsum("fco,or->fcr", feature, head_weight, preferred_element_type=jnp.float32)
    return (detections, scores)


def solution(mesh):
    finer = Mesh(mesh.devices.reshape(mesh.shape["phase"], 4, 16), ("phase", "wide_0", "wide_1"))
    placed = (
        P(None, None, WIDE),
        P("phase", None, None),
        P(),
        P("phase", None, WIDE),
        P("phase", WIDE),
        P("phase", WIDE),
        P("phase", WIDE),
        P(),
        P(),
        P(),
    )
    return jax.shard_map(
        local,
        mesh=finer,
        in_specs=placed,
        out_specs=(P("phase", WIDE, None), P("phase", None, WIDE)),
        check_vma=False,
    )
```

profile of v0, /device:TPU:6, one launch (start us, length us, event | category | flops | bytes accessed | tf_op | source)
XLA Modules:
  0.0 344.1 jit_solution(6971880708646652760)
XLA Ops:
  7.2 0.7 all-gather.5.cloned.1.call-update
  7.9 0.8 copy-done
  8.8 0.1 copy.38
  8.9 67.4 %all-gather.5.cloned.1.call-done = bf16[8,256,2304]{2,1,0:T(8,128)(2,1)} async-done(((bf16[1,256,2304]{2,1,0:T(8,128)(2,1)}), bf16[8,256,2304]{2,1,0:T(8,128)(2,1)}) %all-gather.5.cloned.1.call-update) | async-done | bytes 9437200 | tf_op jit(solution)/shard_map/all_gather | solution.py:105
  76.3 112.8 %while.18 = (s32[]{:T(128)}, bf16[2,256,256]{1,2,0:T(8,128)(2,1)S(1)}, bf16[8,256,2304]{2,1,0:T(8,128)(2,1)}, s32[]{:T(128)}) while((s32[]{:T(128)}, bf16[2,256,256]{1,2,0:T(8,128)(2,1)S(1)}, bf16[8,256,2304]{2,1,0:T(8,128)(2,1)}, s32[]{:T(128)}) %tuple.72), condition=%wide.region_1.2_spmd, body=%wide.region_0.1_spmd.sunk | while | flops 608062720 | bytes 11410577 | solution.py:111
  76.3 6.2 %collective-permute-start = (bf16[2,256,64]{1,2,0:T(8,128)(2,1)S(1)}, bf16[2,256,64]{1,2,0:T(8,128)(2,1)S(1)}, u32[]{:S(2)}, u32[]{:S(2)}) collective-permute-start(bf16[2,256,64]{1,2,0:T(8,128)(2,1)S(1)} %get-tuple-element.195), channel_id=1, source_target_pairs={{1,0},{2,1},{3,2},{4,3},{5,4},{6,5},{7,6},{8,7},{9,8},{10,9},{11,1... | collective-permute-start | bytes 196616 | tf_op jit(solution)/shard_map/while/body/eval_jaxpr/ppermute | solution.py:23
  82.6 1.9 collective-permute-start.1
  84.5 6.3 %collective-permute-done.1 = bf16[2,256,64]{1,2,0:T(8,128)(2,1)S(1)} collective-permute-done((bf16[2,256,64]{1,2,0:T(8,128)(2,1)S(1)}, bf16[2,256,64]{1,2,0:T(8,128)(2,1)S(1)}, u32[]{:S(2)}, u32[]{:S(2)}) %collective-permute-start.1) | collective-permute-done | bytes 65568 | tf_op jit(solution)/shard_map/while/body/eval_jaxpr/ppermute | solution.py:22
  91.5 0.1 constant_dynamic-update-slice_fusion.18
  92.1 2.1 fusion.91
  94.2 1.9 collective-permute-start
  96.1 3.9 %collective-permute-start.1 = (bf16[2,256,64]{1,2,0:T(8,128)(2,1)S(1)}, bf16[2,256,64]{1,2,0:T(8,128)(2,1)S(1)}, u32[]{:S(2)}, u32[]{:S(2)}) collective-permute-start(bf16[2,256,64]{1,2,0:T(8,128)(2,1)S(1)} %get-tuple-element.196), channel_id=1, source_target_pairs={{0,1},{1,2},{2,3},{3,4},{4,5},{5,6},{6,7},{7,8},{8,9},{9,10},{10,1... | collective-permute-start | bytes 196616 | tf_op jit(solution)/shard_map/while/body/eval_jaxpr/ppermute | solution.py:22
  100.1 4.3 %collective-permute-done.1 = bf16[2,256,64]{1,2,0:T(8,128)(2,1)S(1)} collective-permute-done((bf16[2,256,64]{1,2,0:T(8,128)(2,1)S(1)}, bf16[2,256,64]{1,2,0:T(8,128)(2,1)S(1)}, u32[]{:S(2)}, u32[]{:S(2)}) %collective-permute-start.1) | collective-permute-done | bytes 65568 | tf_op jit(solution)/shard_map/while/body/eval_jaxpr/ppermute | solution.py:22
  105.6 2.1 fusion.91
  107.8 1.9 collective-permute-start
  109.7 3.9 %collective-permute-start.1 = (bf16[2,256,64]{1,2,0:T(8,128)(2,1)S(1)}, bf16[2,256,64]{1,2,0:T(8,128)(2,1)S(1)}, u32[]{:S(2)}, u32[]{:S(2)}) collective-permute-start(bf16[2,256,64]{1,2,0:T(8,128)(2,1)S(1)} %get-tuple-element.196), channel_id=1, source_target_pairs={{0,1},{1,2},{2,3},{3,4},{4,5},{5,6},{6,7},{7,8},{8,9},{9,10},{10,1... | collective-permute-start | bytes 196616 | tf_op jit(solution)/shard_map/while/body/eval_jaxpr/ppermute | solution.py:22
  113.7 4.3 %collective-permute-done.1 = bf16[2,256,64]{1,2,0:T(8,128)(2,1)S(1)} collective-permute-done((bf16[2,256,64]{1,2,0:T(8,128)(2,1)S(1)}, bf16[2,256,64]{1,2,0:T(8,128)(2,1)S(1)}, u32[]{:S(2)}, u32[]{:S(2)}) %collective-permute-start.1) | collective-permute-done | bytes 65568 | tf_op jit(solution)/shard_map/while/body/eval_jaxpr/ppermute | solution.py:22
  118.6 0.1 constant_dynamic-update-slice_fusion.18
  119.2 2.1 fusion.91
  121.3 1.9 collective-permute-start
  123.3 3.9 %collective-permute-start.1 = (bf16[2,256,64]{1,2,0:T(8,128)(2,1)S(1)}, bf16[2,256,64]{1,2,0:T(8,128)(2,1)S(1)}, u32[]{:S(2)}, u32[]{:S(2)}) collective-permute-start(bf16[2,256,64]{1,2,0:T(8,128)(2,1)S(1)} %get-tuple-element.196), channel_id=1, source_target_pairs={{0,1},{1,2},{2,3},{3,4},{4,5},{5,6},{6,7},{7,8},{8,9},{9,10},{10,1... | collective-permute-start | bytes 196616 | tf_op jit(solution)/shard_map/while/body/eval_jaxpr/ppermute | solution.py:22
  127.2 4.3 %collective-permute-done.1 = bf16[2,256,64]{1,2,0:T(8,128)(2,1)S(1)} collective-permute-done((bf16[2,256,64]{1,2,0:T(8,128)(2,1)S(1)}, bf16[2,256,64]{1,2,0:T(8,128)(2,1)S(1)}, u32[]{:S(2)}, u32[]{:S(2)}) %collective-permute-start.1) | collective-permute-done | bytes 65568 | tf_op jit(solution)/shard_map/while/body/eval_jaxpr/ppermute | solution.py:22
  132.2 0.1 constant_dynamic-update-slice_fusion.18
  132.8 2.1 fusion.91
  134.9 1.9 collective-permute-start
  136.8 3.9 %collective-permute-start.1 = (bf16[2,256,64]{1,2,0:T(8,128)(2,1)S(1)}, bf16[2,256,64]{1,2,0:T(8,128)(2,1)S(1)}, u32[]{:S(2)}, u32[]{:S(2)}) collective-permute-start(bf16[2,256,64]{1,2,0:T(8,128)(2,1)S(1)} %get-tuple-element.196), channel_id=1, source_target_pairs={{0,1},{1,2},{2,3},{3,4},{4,5},{5,6},{6,7},{7,8},{8,9},{9,10},{10,1... | collective-permute-start | bytes 196616 | tf_op jit(solution)/shard_map/while/body/eval_jaxpr/ppermute | solution.py:22
  140.8 4.3 %collective-permute-done.1 = bf16[2,256,64]{1,2,0:T(8,128)(2,1)S(1)} collective-permute-done((bf16[2,256,64]{1,2,0:T(8,128)(2,1)S(1)}, bf16[2,256,64]{1,2,0:T(8,128)(2,1)S(1)}, u32[]{:S(2)}, u32[]{:S(2)}) %collective-permute-start.1) | collective-permute-done | bytes 65568 | tf_op jit(solution)/shard_map/while/body/eval_jaxpr/ppermute | solution.py:22
  145.7 0.1 constant_dynamic-update-slice_fusion.18
  146.4 2.1 fusion.91
  148.5 1.9 collective-permute-start
  150.4 3.9 %collective-permute-start.1 = (bf16[2,256,64]{1,2,0:T(8,128)(2,1)S(1)}, bf16[2,256,64]{1,2,0:T(8,128)(2,1)S(1)}, u32[]{:S(2)}, u32[]{:S(2)}) collective-permute-start(bf16[2,256,64]{1,2,0:T(8,128)(2,1)S(1)} %get-tuple-element.196), channel_id=1, source_target_pairs={{0,1},{1,2},{2,3},{3,4},{4,5},{5,6},{6,7},{7,8},{8,9},{9,10},{10,1... | collective-permute-start | bytes 196616 | tf_op jit(solution)/shard_map/while/body/eval_jaxpr/ppermute | solution.py:22
  154.4 4.3 %collective-permute-done.1 = bf16[2,256,64]{1,2,0:T(8,128)(2,1)S(1)} collective-permute-done((bf16[2,256,64]{1,2,0:T(8,128)(2,1)S(1)}, bf16[2,256,64]{1,2,0:T(8,128)(2,1)S(1)}, u32[]{:S(2)}, u32[]{:S(2)}) %collective-permute-start.1) | collective-permute-done | bytes 65568 | tf_op jit(solution)/shard_map/while/body/eval_jaxpr/ppermute | solution.py:22
  159.3 0.1 constant_dynamic-update-slice_fusion.18
  159.9 2.1 fusion.91
  162.1 1.9 collective-permute-start
  164.0 3.9 %collective-permute-start.1 = (bf16[2,256,64]{1,2,0:T(8,128)(2,1)S(1)}, bf16[2,256,64]{1,2,0:T(8,128)(2,1)S(1)}, u32[]{:S(2)}, u32[]{:S(2)}) collective-permute-start(bf16[2,256,64]{1,2,0:T(8,128)(2,1)S(1)} %get-tuple-element.196), channel_id=1, source_target_pairs={{0,1},{1,2},{2,3},{3,4},{4,5},{5,6},{6,7},{7,8},{8,9},{9,10},{10,1... | collective-permute-start | bytes 196616 | tf_op jit(solution)/shard_map/while/body/eval_jaxpr/ppermute | solution.py:22
  167.9 4.3 %collective-permute-done.1 = bf16[2,256,64]{1,2,0:T(8,128)(2,1)S(1)} collective-permute-done((bf16[2,256,64]{1,2,0:T(8,128)(2,1)S(1)}, bf16[2,256,64]{1,2,0:T(8,128)(2,1)S(1)}, u32[]{:S(2)}, u32[]{:S(2)}) %collective-permute-start.1) | collective-permute-done | bytes 65568 | tf_op jit(solution)/shard_map/while/body/eval_jaxpr/ppermute | solution.py:22
  172.9 0.1 constant_dynamic-update-slice_fusion.18
  173.5 2.1 fusion.91
  175.6 1.9 collective-permute-start
  177.5 3.9 %collective-permute-start.1 = (bf16[2,256,64]{1,2,0:T(8,128)(2,1)S(1)}, bf16[2,256,64]{1,2,0:T(8,128)(2,1)S(1)}, u32[]{:S(2)}, u32[]{:S(2)}) collective-permute-start(bf16[2,256,64]{1,2,0:T(8,128)(2,1)S(1)} %get-tuple-element.196), channel_id=1, source_target_pairs={{0,1},{1,2},{2,3},{3,4},{4,5},{5,6},{6,7},{7,8},{8,9},{9,10},{10,1... | collective-permute-start | bytes 196616 | tf_op jit(solution)/shard_map/while/body/eval_jaxpr/ppermute | solution.py:22
  181.5 4.3 %collective-permute-done.1 = bf16[2,256,64]{1,2,0:T(8,128)(2,1)S(1)} collective-permute-done((bf16[2,256,64]{1,2,0:T(8,128)(2,1)S(1)}, bf16[2,256,64]{1,2,0:T(8,128)(2,1)S(1)}, u32[]{:S(2)}, u32[]{:S(2)}) %collective-permute-start.1) | collective-permute-done | bytes 65568 | tf_op jit(solution)/shard_map/while/body/eval_jaxpr/ppermute | solution.py:22
  187.1 2.1 fusion.91
  189.2 0.2 fusion.54
  189.4 0.7 fusion.58
  190.0 1.2 broadcast_in_dim.201
  191.2 5.4 %all-to-all-start = ((bf16[64,2,11,256]{3,1,2,0:T(2,128)(2,1)}), bf16[64,2,11,256]{3,1,2,0:T(2,128)(2,1)S(1)}, u32[]{:S(2)}, u32[]{:S(2)}) async-start(bf16[64,2,11,256]{3,1,2,0:T(2,128)(2,1)} %broadcast_in_dim.201), calls=%async_computation | async-start | bytes 1441792 | tf_op jit(solution)/shard_map/all_to_all | solution.py:36
  196.8 29.8 %all-to-all-done = bf16[64,2,11,256]{3,1,2,0:T(2,128)(2,1)S(1)} async-done(((bf16[64,2,11,256]{3,1,2,0:T(2,128)(2,1)}), bf16[64,2,11,256]{3,1,2,0:T(2,128)(2,1)S(1)}, u32[]{:S(2)}, u32[]{:S(2)}) %all-to-all-start) | async-done | bytes 720928 | tf_op jit(solution)/shard_map/all_to_all | solution.py:36
  226.6 0.1 copy.36
  226.7 1.5 reshape.132
  228.2 6.5 %fusion.35 = f32[2,11,256]{2,1,0:T(8,128)S(1)} fusion(bf16[2,11,16384]{2,1,0:T(8,128)(2,1)} %reshape.132, s32[2,256]{1,0:T(2,128)S(1)} %copy-done.7), kind=kOutput, calls=%fused_computation.59 | convolution fusion | flops 192954880 | bytes 745472 | tf_op jit(solution)/shard_map/fkn,fnp->fkp/dot_general | solution.py:119
  234.8 0.3 fusion.30
  235.1 13.0 %all_gather.18 = bf16[2,64,1024]{2,1,0:T(8,128)(2,1)} all-gather(bf16[2,64,256]{2,1,0:T(8,128)(2,1)S(1)} %fusion.30), channel_id=1, replica_groups=mesh['phase'=8,'wide_0'=4,'wide_1'=16] {'wide_0'}, dimensions={2}, use_global_device_ids=true | all-gather | bytes 327680 | tf_op jit(solution)/shard_map/all_gather | solution.py:48
  248.1 10.2 %all-gather = s32[2,1024]{1,0:T(2,128)S(1)} all-gather(s32[2,256]{1,0:T(2,128)S(1)} %copy-done.4), channel_id=2, replica_groups=mesh['phase'=8,'wide_0'=4,'wide_1'=16] {'wide_0'}, dimensions={1}, use_global_device_ids=true | all-gather | bytes 10240 | tf_op jit(solution)/shard_map/all_gather | solution.py:48
  258.3 29.0 %all-gather.1 = s32[2,16384]{1,0:T(2,128)S(1)} all-gather(s32[2,1024]{1,0:T(2,128)S(1)} %all-gather), channel_id=3, replica_groups=mesh['phase'=8,'wide_0'=4,'wide_1'=16] {'wide_1'}, dimensions={1}, use_global_device_ids=true | all-gather | bytes 139264 | tf_op jit(solution)/shard_map/all_gather | solution.py:48
  287.4 31.9 %all-gather.7.cloned.1.call-done = bf16[2,64,16384]{2,1,0:T(8,128)(2,1)} async-done(((bf16[2,64,1024]{2,1,0:T(8,128)(2,1)}), bf16[2,64,16384]{2,1,0:T(8,128)(2,1)}) %all-gather.7.cloned.1.call-update) | async-done | bytes 4194320 | tf_op jit(solution)/shard_map/all_gather | solution.py:48
  319.3 6.7 %fusion.31 = bf16[2,128,64]{1,2,0:T(8,128)(2,1)S(1)} fusion(bf16[2,64,16384]{2,1,0:T(8,128)(2,1)} %all-gather.7.cloned.1.call-done, s32[2,16384]{1,0:T(2,128)S(1)} %broadcast_subtract_fusion), kind=kOutput, calls=%fused_computation.55 | convolution fusion | flops 541081600 | bytes 4358144 | tf_op jit(solution)/shard_map/fjp,fpc->cfj/dot_general | solution.py:134
  326.1 2.6 collective-permute-start.2
  328.6 5.4 %collective-permute-start.3 = (bf16[128,128]{0,1:T(8,128)(2,1)S(1)}, bf16[128,128]{0,1:T(8,128)(2,1)S(1)}, u32[]{:S(2)}, u32[]{:S(2)}) collective-permute-start(bf16[128,128]{0,1:T(8,128)(2,1)S(1)} %bitcast.77), channel_id=1, source_target_pairs={{1,0},{2,1},{3,2},{4,3},{5,4},{6,5},{7,6},{8,7},{9,8},{10,9},{11,1... | collective-permute-start | bytes 98312 | tf_op jit(solution)/shard_map/ppermute | solution.py:23
  334.1 1.6 collective-permute-done.3
  335.6 0.1 fusion.42
  335.7 0.2 fusion.48
  336.1 0.5 fusion.27
  336.6 0.6 copy.33
  (173 shorter events, 9.2 us)
Async XLA Ops:
  7.2 1.6 copy-start
  7.2 69.1 %all-gather.5.cloned.1.call-start = ((), (), s32[]{:S(2)}) async-start(), calls=%async_computation.1 | async-start | bytes 10616832 | tf_op jit(solution)/shard_map/all_gather | solution.py:105
  76.3 112.9 %copy-start.3 = (bf16[11,256]{1,0:T(8,128)(2,1)S(1)}, bf16[11,256]{1,0:T(8,128)(2,1)}, u32[]{:S(2)}) copy-start(bf16[11,256]{1,0:T(8,128)(2,1)} %param.14) | copy-start | bytes 16900
  76.3 14.5 %collective-permute-start = (bf16[2,256,64]{1,2,0:T(8,128)(2,1)S(1)}, bf16[2,256,64]{1,2,0:T(8,128)(2,1)S(1)}, u32[]{:S(2)}, u32[]{:S(2)}) collective-permute-start(bf16[2,256,64]{1,2,0:T(8,128)(2,1)S(1)} %get-tuple-element.195), channel_id=1, source_target_pairs={{1,0},{2,1},{3,2},{4,3},{5,4},{6,5},{7,6},{8,7},{9,8},{10,9},{11,1... | collective-permute-start | bytes 196616 | tf_op jit(solution)/shard_map/while/body/eval_jaxpr/ppermute | solution.py:23
  82.6 8.3 %collective-permute-start.1 = (bf16[2,256,64]{1,2,0:T(8,128)(2,1)S(1)}, bf16[2,256,64]{1,2,0:T(8,128)(2,1)S(1)}, u32[]{:S(2)}, u32[]{:S(2)}) collective-permute-start(bf16[2,256,64]{1,2,0:T(8,128)(2,1)S(1)} %get-tuple-element.196), channel_id=1, source_target_pairs={{0,1},{1,2},{2,3},{3,4},{4,5},{5,6},{6,7},{7,8},{8,9},{9,10},{10,1... | collective-permute-start | bytes 196616 | tf_op jit(solution)/shard_map/while/body/eval_jaxpr/ppermute | solution.py:22
  94.2 10.2 %collective-permute-start = (bf16[2,256,64]{1,2,0:T(8,128)(2,1)S(1)}, bf16[2,256,64]{1,2,0:T(8,128)(2,1)S(1)}, u32[]{:S(2)}, u32[]{:S(2)}) collective-permute-start(bf16[2,256,64]{1,2,0:T(8,128)(2,1)S(1)} %get-tuple-element.195), channel_id=1, source_target_pairs={{1,0},{2,1},{3,2},{4,3},{5,4},{6,5},{7,6},{8,7},{9,8},{10,9},{11,1... | collective-permute-start | bytes 196616 | tf_op jit(solution)/shard_map/while/body/eval_jaxpr/ppermute | solution.py:23
  96.1 8.3 %collective-permute-start.1 = (bf16[2,256,64]{1,2,0:T(8,128)(2,1)S(1)}, bf16[2,256,64]{1,2,0:T(8,128)(2,1)S(1)}, u32[]{:S(2)}, u32[]{:S(2)}) collective-permute-start(bf16[2,256,64]{1,2,0:T(8,128)(2,1)S(1)} %get-tuple-element.196), channel_id=1, source_target_pairs={{0,1},{1,2},{2,3},{3,4},{4,5},{5,6},{6,7},{7,8},{8,9},{9,10},{10,1... | collective-permute-start | bytes 196616 | tf_op jit(solution)/shard_map/while/body/eval_jaxpr/ppermute | solution.py:22
  107.8 10.2 %collective-permute-start = (bf16[2,256,64]{1,2,0:T(8,128)(2,1)S(1)}, bf16[2,256,64]{1,2,0:T(8,128)(2,1)S(1)}, u32[]{:S(2)}, u32[]{:S(2)}) collective-permute-start(bf16[2,256,64]{1,2,0:T(8,128)(2,1)S(1)} %get-tuple-element.195), channel_id=1, source_target_pairs={{1,0},{2,1},{3,2},{4,3},{5,4},{6,5},{7,6},{8,7},{9,8},{10,9},{11,1... | collective-permute-start | bytes 196616 | tf_op jit(solution)/shard_map/while/body/eval_jaxpr/ppermute | solution.py:23
  109.7 8.3 %collective-permute-start.1 = (bf16[2,256,64]{1,2,0:T(8,128)(2,1)S(1)}, bf16[2,256,64]{1,2,0:T(8,128)(2,1)S(1)}, u32[]{:S(2)}, u32[]{:S(2)}) collective-permute-start(bf16[2,256,64]{1,2,0:T(8,128)(2,1)S(1)} %get-tuple-element.196), channel_id=1, source_target_pairs={{0,1},{1,2},{2,3},{3,4},{4,5},{5,6},{6,7},{7,8},{8,9},{9,10},{10,1... | collective-permute-start | bytes 196616 | tf_op jit(solution)/shard_map/while/body/eval_jaxpr/ppermute | solution.py:22
  121.3 10.2 %collective-permute-start = (bf16[2,256,64]{1,2,0:T(8,128)(2,1)S(1)}, bf16[2,256,64]{1,2,0:T(8,128)(2,1)S(1)}, u32[]{:S(2)}, u32[]{:S(2)}) collective-permute-start(bf16[2,256,64]{1,2,0:T(8,128)(2,1)S(1)} %get-tuple-element.195), channel_id=1, source_target_pairs={{1,0},{2,1},{3,2},{4,3},{5,4},{6,5},{7,6},{8,7},{9,8},{10,9},{11,1... | collective-permute-start | bytes 196616 | tf_op jit(solution)/shard_map/while/body/eval_jaxpr/ppermute | solution.py:23
  123.3 8.3 %collective-permute-start.1 = (bf16[2,256,64]{1,2,0:T(8,128)(2,1)S(1)}, bf16[2,256,64]{1,2,0:T(8,128)(2,1)S(1)}, u32[]{:S(2)}, u32[]{:S(2)}) collective-permute-start(bf16[2,256,64]{1,2,0:T(8,128)(2,1)S(1)} %get-tuple-element.196), channel_id=1, source_target_pairs={{0,1},{1,2},{2,3},{3,4},{4,5},{5,6},{6,7},{7,8},{8,9},{9,10},{10,1... | collective-permute-start | bytes 196616 | tf_op jit(solution)/shard_map/while/body/eval_jaxpr/ppermute | solution.py:22
  134.9 10.2 %collective-permute-start = (bf16[2,256,64]{1,2,0:T(8,128)(2,1)S(1)}, bf16[2,256,64]{1,2,0:T(8,128)(2,1)S(1)}, u32[]{:S(2)}, u32[]{:S(2)}) collective-permute-start(bf16[2,256,64]{1,2,0:T(8,128)(2,1)S(1)} %get-tuple-element.195), channel_id=1, source_target_pairs={{1,0},{2,1},{3,2},{4,3},{5,4},{6,5},{7,6},{8,7},{9,8},{10,9},{11,1... | collective-permute-start | bytes 196616 | tf_op jit(solution)/shard_map/while/body/eval_jaxpr/ppermute | solution.py:23
  136.8 8.3 %collective-permute-start.1 = (bf16[2,256,64]{1,2,0:T(8,128)(2,1)S(1)}, bf16[2,256,64]{1,2,0:T(8,128)(2,1)S(1)}, u32[]{:S(2)}, u32[]{:S(2)}) collective-permute-start(bf16[2,256,64]{1,2,0:T(8,128)(2,1)S(1)} %get-tuple-element.196), channel_id=1, source_target_pairs={{0,1},{1,2},{2,3},{3,4},{4,5},{5,6},{6,7},{7,8},{8,9},{9,10},{10,1... | collective-permute-start | bytes 196616 | tf_op jit(solution)/shard_map/while/body/eval_jaxpr/ppermute | solution.py:22
  148.5 10.2 %collective-permute-start = (bf16[2,256,64]{1,2,0:T(8,128)(2,1)S(1)}, bf16[2,256,64]{1,2,0:T(8,128)(2,1)S(1)}, u32[]{:S(2)}, u32[]{:S(2)}) collective-permute-start(bf16[2,256,64]{1,2,0:T(8,128)(2,1)S(1)} %get-tuple-element.195), channel_id=1, source_target_pairs={{1,0},{2,1},{3,2},{4,3},{5,4},{6,5},{7,6},{8,7},{9,8},{10,9},{11,1... | collective-permute-start | bytes 196616 | tf_op jit(solution)/shard_map/while/body/eval_jaxpr/ppermute | solution.py:23
  150.4 8.3 %collective-permute-start.1 = (bf16[2,256,64]{1,2,0:T(8,128)(2,1)S(1)}, bf16[2,256,64]{1,2,0:T(8,128)(2,1)S(1)}, u32[]{:S(2)}, u32[]{:S(2)}) collective-permute-start(bf16[2,256,64]{1,2,0:T(8,128)(2,1)S(1)} %get-tuple-element.196), channel_id=1, source_target_pairs={{0,1},{1,2},{2,3},{3,4},{4,5},{5,6},{6,7},{7,8},{8,9},{9,10},{10,1... | collective-permute-start | bytes 196616 | tf_op jit(solution)/shard_map/while/body/eval_jaxpr/ppermute | solution.py:22
  162.1 10.2 %collective-permute-start = (bf16[2,256,64]{1,2,0:T(8,128)(2,1)S(1)}, bf16[2,256,64]{1,2,0:T(8,128)(2,1)S(1)}, u32[]{:S(2)}, u32[]{:S(2)}) collective-permute-start(bf16[2,256,64]{1,2,0:T(8,128)(2,1)S(1)} %get-tuple-element.195), channel_id=1, source_target_pairs={{1,0},{2,1},{3,2},{4,3},{5,4},{6,5},{7,6},{8,7},{9,8},{10,9},{11,1... | collective-permute-start | bytes 196616 | tf_op jit(solution)/shard_map/while/body/eval_jaxpr/ppermute | solution.py:23
  164.0 8.3 %collective-permute-start.1 = (bf16[2,256,64]{1,2,0:T(8,128)(2,1)S(1)}, bf16[2,256,64]{1,2,0:T(8,128)(2,1)S(1)}, u32[]{:S(2)}, u32[]{:S(2)}) collective-permute-start(bf16[2,256,64]{1,2,0:T(8,128)(2,1)S(1)} %get-tuple-element.196), channel_id=1, source_target_pairs={{0,1},{1,2},{2,3},{3,4},{4,5},{5,6},{6,7},{7,8},{8,9},{9,10},{10,1... | collective-permute-start | bytes 196616 | tf_op jit(solution)/shard_map/while/body/eval_jaxpr/ppermute | solution.py:22
  175.6 10.2 %collective-permute-start = (bf16[2,256,64]{1,2,0:T(8,128)(2,1)S(1)}, bf16[2,256,64]{1,2,0:T(8,128)(2,1)S(1)}, u32[]{:S(2)}, u32[]{:S(2)}) collective-permute-start(bf16[2,256,64]{1,2,0:T(8,128)(2,1)S(1)} %get-tuple-element.195), channel_id=1, source_target_pairs={{1,0},{2,1},{3,2},{4,3},{5,4},{6,5},{7,6},{8,7},{9,8},{10,9},{11,1... | collective-permute-start | bytes 196616 | tf_op jit(solution)/shard_map/while/body/eval_jaxpr/ppermute | solution.py:23
  177.5 8.3 %collective-permute-start.1 = (bf16[2,256,64]{1,2,0:T(8,128)(2,1)S(1)}, bf16[2,256,64]{1,2,0:T(8,128)(2,1)S(1)}, u32[]{:S(2)}, u32[]{:S(2)}) collective-permute-start(bf16[2,256,64]{1,2,0:T(8,128)(2,1)S(1)} %get-tuple-element.196), channel_id=1, source_target_pairs={{0,1},{1,2},{2,3},{3,4},{4,5},{5,6},{6,7},{7,8},{8,9},{9,10},{10,1... | collective-permute-start | bytes 196616 | tf_op jit(solution)/shard_map/while/body/eval_jaxpr/ppermute | solution.py:22
  189.2 7.6 %copy-start.8 = (s32[2,1]{0,1:T(1,128)S(1)}, s32[2,1]{0,1:T(1,128)}, u32[]{:S(2)}) copy-start(s32[2,1]{0,1:T(1,128)} %param.18) | copy-start | bytes 28
  191.2 36.9 %copy-start.7 = (s32[2,256]{1,0:T(2,128)S(1)}, s32[2,256]{1,0:T(2,128)}, u32[]{:S(2)}) copy-start(s32[2,256]{1,0:T(2,128)} %param.16) | copy-start | bytes 6148
  191.2 35.3 %all-to-all-start = ((bf16[64,2,11,256]{3,1,2,0:T(2,128)(2,1)}), bf16[64,2,11,256]{3,1,2,0:T(2,128)(2,1)S(1)}, u32[]{:S(2)}, u32[]{:S(2)}) async-start(bf16[64,2,11,256]{3,1,2,0:T(2,128)(2,1)} %broadcast_in_dim.201), calls=%async_computation | async-start | bytes 1441792 | tf_op jit(solution)/shard_map/all_to_all | solution.py:36
  196.7 122.6 %all-gather.7.cloned.1.call-start = ((), (), s32[]{:S(2)}) async-start(), calls=%async_computation.2 | async-start | bytes 4456448 | tf_op jit(solution)/shard_map/all_gather | solution.py:48
  228.2 6.6 %copy-start.5 = (f32[2,4,256]{2,1,0:T(4,128)S(1)}, f32[2,4,256]{2,1,0:T(4,128)}, u32[]{:S(2)}) copy-start(f32[2,4,256]{2,1,0:T(4,128)} %param.15) | copy-start | bytes 24580
  228.2 6.6 %copy-start.6 = (f32[64,15]{0,1:T(8,128)S(1)}, f32[64,15]{0,1:T(8,128)}, u32[]{:S(2)}) copy-start(f32[64,15]{0,1:T(8,128)} %param.19) | copy-start | bytes 11524
  228.2 19.9 %copy-start.4 = (s32[2,256]{1,0:T(2,128)S(1)}, s32[2,256]{1,0:T(2,128)}, u32[]{:S(2)}) copy-start(s32[2,256]{1,0:T(2,128)} %param.17) | copy-start | bytes 6148
  287.4 48.7 %copy-start.1 = (bf16[576,384]{1,0:T(8,128)(2,1)S(1)}, bf16[576,384]{1,0:T(8,128)(2,1)}, u32[]{:S(2)}) copy-start(bf16[576,384]{1,0:T(8,128)(2,1)} %param.20) | copy-start | bytes 1327108
  287.4 48.7 %copy-start.2 = (bf16[384,20]{0,1:T(8,128)(2,1)S(1)}, bf16[384,20]{0,1:T(8,128)(2,1)}, u32[]{:S(2)}) copy-start(bf16[384,20]{0,1:T(8,128)(2,1)} %param.21) | copy-start | bytes 46084
  326.1 8.0 %collective-permute-start.2 = (bf16[128,128]{0,1:T(8,128)(2,1)S(1)}, bf16[128,128]{0,1:T(8,128)(2,1)S(1)}, u32[]{:S(2)}, u32[]{:S(2)}) collective-permute-start(bf16[128,128]{0,1:T(8,128)(2,1)S(1)} %bitcast.76), channel_id=1, source_target_pairs={{0,1},{1,2},{2,3},{3,4},{4,5},{5,6},{6,7},{7,8},{8,9},{9,10},{10,1... | collective-permute-start | bytes 98312 | tf_op jit(solution)/shard_map/ppermute | solution.py:22
  328.6 7.0 %collective-permute-start.3 = (bf16[128,128]{0,1:T(8,128)(2,1)S(1)}, bf16[128,128]{0,1:T(8,128)(2,1)S(1)}, u32[]{:S(2)}, u32[]{:S(2)}) collective-permute-start(bf16[128,128]{0,1:T(8,128)(2,1)S(1)} %bitcast.77), channel_id=1, source_target_pairs={{1,0},{2,1},{3,2},{4,3},{5,4},{6,5},{7,6},{8,7},{9,8},{10,9},{11,1... | collective-permute-start | bytes 98312 | tf_op jit(solution)/shard_map/ppermute | solution.py:23
Sparse Core Ops, SparseCore 0:
  10.1 66.1 all-gather.4
  248.2 71.0 all-gather.6
where the time goes:
time: 345 us; the launch traced here: 344 us
  waiting for transfers between devices  168 us (49%)
  starting transfers between devices  62.5 us (18%)
  blocking collectives  52.2 us (15%)
  matrix products  31 us (9%)
  between operations  14.3 us (4%)
  other arithmetic  10.2 us (3%)
  local copies, waits for them, and re-layouts  4.91 us (1%)
    all_gather x1, waiting for transfers between devices, local(): weights = lax.all_gather(conv_weight, 'phase', axis=0, tiled=True)  67.4 us
    all_gather x3, blocking collectives, whole_of(): filled = lax.all_gather(filled, axes[number], axis=dim, tiled=True)  52.2 us
    ppermute x9, waiting for transfers between devices, padded_2(): before = lax.ppermute(last, axis, up)  36.4 us
    ppermute x9, starting transfers between devices, padded_2(): before = lax.ppermute(last, axis, up)  31.9 us
    all_gather x1, waiting for transfers between devices, whole_of(): filled = lax.all_gather(filled, axes[number], axis=dim, tiled=True)  31.9 us
    all_to_all x1, waiting for transfers between devices, copy_for_each(): lax.all_to_all(jnp.broadcast_to(value[None], (devices, *value.shape)), ax...  29.8 us
    ppermute x9, starting transfers between devices, padded_2(): after = lax.ppermute(first, axis, down)  25.1 us
    dot_general x8, matrix products, image_layer(): jnp.einsum('ok,fkp->fop', weight, stacked, preferred_element_type=jnp.flo...  16.7 us
  transfers between devices with their start and end apart: 21, of which 12 were waited for; matrix products, arithmetic and copies ran while one was open for 0% of the time, Pallas kernels for 0%

commit v1 on v0

--- a/solution.py
+++ b/solution.py
@@ -10,6 +10,11 @@
 BEV_W = 128
 CELLS_DEV = 128
 WIDE = ("wide_0", "wide_1")
+
+
+def gather_from_all(x, axis, dim):
+    copies = jnp.concatenate([x] * lax.axis_size(axis), axis=dim)
+    return lax.all_to_all(copies, axis, dim, dim, tiled=True)
 
 
 def padded_2(value, sides, width):
@@ -102,7 +107,7 @@
     phase_now = lax.axis_index("phase")
     phases = lax.axis_size("phase")
     own_frames = point_feats.shape[0]
-    weights = lax.all_gather(conv_weight, "phase", axis=0, tiled=True)
+    weights = gather_from_all(conv_weight, "phase", 0)
     start_maps = lax.dynamic_slice_in_dim(image, phase_now * own_frames, own_frames, 0)
 
     def layer_step(layer, activation):

time: 345 us -> 397 us (1.15)
  waiting for transfers between devices: 168 us -> 204 us
  starting transfers between devices: 62.5 us -> 73 us
  local copies, waits for them, and re-layouts: 4.91 us -> 9.71 us
    all_to_all x0 -> x1, waiting for transfers between devices: none -> 106 us  [gather_from_all(): return lax.all_to_all(copies, axis, dim, dim, tiled=True)]
    all_gather x1 -> x0, waiting for transfers between devices: 67.4 us -> none  [local(): weights = lax.all_gather(conv_weight, 'phase', axis=0, tiled=True)]
    concatenate x0 -> x1, local copies, waits for them, and re-layouts: none -> 5.66 us  [gather_from_all(): copies = jnp.concatenate([x] * lax.axis_size(axis), axis=dim)]
    ppermute x9, starting transfers between devices: 25.1 us -> 30.6 us  [padded_2(): after = lax.ppermute(first, axis, down)]
    all_to_all x0 -> x1, starting transfers between devices: none -> 5.06 us  [gather_from_all(): return lax.all_to_all(copies, axis, dim, dim, tiled=True)]
where the time goes in v1:
time: 397 us; the launch traced here: 395 us
  waiting for transfers between devices  204 us (51%)
  starting transfers between devices  73 us (18%)
  blocking collectives  51.9 us (13%)
  matrix products  31 us (8%)
  between operations  14.3 us (4%)
  other arithmetic  10.2 us (3%)
  local copies, waits for them, and re-layouts  9.71 us (2%)
    all_to_all x1, waiting for transfers between devices, gather_from_all(): return lax.all_to_all(copies, axis, dim, dim, tiled=True)  106 us
    all_gather x3, blocking collectives, whole_of(): filled = lax.all_gather(filled, axes[number], axis=dim, tiled=True)  51.9 us
    ppermute x9, waiting for transfers between devices, padded_2(): before = lax.ppermute(last, axis, up)  36.4 us
    ppermute x9, starting transfers between devices, padded_2(): before = lax.ppermute(last, axis, up)  31.9 us
    all_gather x1, waiting for transfers between devices, whole_of(): filled = lax.all_gather(filled, axes[number], axis=dim, tiled=True)  31 us
    ppermute x9, starting transfers between devices, padded_2(): after = lax.ppermute(first, axis, down)  30.6 us
    all_to_all x1, waiting for transfers between devices, copy_for_each(): lax.all_to_all(jnp.broadcast_to(value[None], (devices, *value.shape)), ax...  29.3 us
    dot_general x8, matrix products, image_layer(): jnp.einsum('ok,fkp->fop', weight, stacked, preferred_element_type=jnp.flo...  16.7 us
  transfers between devices with their start and end apart: 21, of which 12 were waited for; matrix products, arithmetic and copies ran while one was open for 0% of the time, Pallas kernels for 0%

profile of v1, /device:TPU:6, one launch (start us, length us, event | category | flops | bytes accessed | tf_op | source)
XLA Modules:
  0.0 395.3 jit_solution(6255621969345528638)
XLA Ops:
  7.2 5.7 %concatenate.86 = bf16[8,256,2304]{2,1,0:T(8,128)(2,1)} broadcast(bf16[256,2304]{1,0:T(8,128)(2,1)} %bitcast.76), dimensions={1,2} | broadcast | bytes 10616832 | tf_op jit(solution)/shard_map/concatenate | solution.py:16
  12.8 5.1 %all-to-all-start = ((bf16[8,256,2304]{2,1,0:T(8,128)(2,1)}), bf16[8,256,2304]{2,1,0:T(8,128)(2,1)}, u32[]{:S(2)}, u32[]{:S(2)}) async-start(bf16[8,256,2304]{2,1,0:T(8,128)(2,1)} %concatenate.86), calls=%async_computation | async-start | bytes 18874368 | tf_op jit(solution)/shard_map/all_to_all | solution.py:17
  18.0 0.1 copy.38
  18.1 105.6 %all-to-all-done = bf16[8,256,2304]{2,1,0:T(8,128)(2,1)} async-done(((bf16[8,256,2304]{2,1,0:T(8,128)(2,1)}), bf16[8,256,2304]{2,1,0:T(8,128)(2,1)}, u32[]{:S(2)}, u32[]{:S(2)}) %all-to-all-start) | async-done | bytes 9437216 | tf_op jit(solution)/shard_map/all_to_all | solution.py:17
  123.7 118.3 %while.18 = (s32[]{:T(128)}, bf16[2,256,256]{1,2,0:T(8,128)(2,1)S(1)}, bf16[8,256,2304]{2,1,0:T(8,128)(2,1)}, s32[]{:T(128)}) while((s32[]{:T(128)}, bf16[2,256,256]{1,2,0:T(8,128)(2,1)S(1)}, bf16[8,256,2304]{2,1,0:T(8,128)(2,1)}, s32[]{:T(128)}) %tuple.72), condition=%wide.region_1.2_spmd, body=%wide.region_0.1_spmd.sunk | while | flops 608062720 | bytes 11410577 | solution.py:116
  123.7 11.7 %collective-permute-start = (bf16[2,256,64]{1,2,0:T(8,128)(2,1)S(1)}, bf16[2,256,64]{1,2,0:T(8,128)(2,1)S(1)}, u32[]{:S(2)}, u32[]{:S(2)}) collective-permute-start(bf16[2,256,64]{1,2,0:T(8,128)(2,1)S(1)} %get-tuple-element.195), channel_id=1, source_target_pairs={{1,0},{2,1},{3,2},{4,3},{5,4},{6,5},{7,6},{8,7},{9,8},{10,9},{11,1... | collective-permute-start | bytes 196616 | tf_op jit(solution)/shard_map/while/body/eval_jaxpr/ppermute | solution.py:28
  135.4 1.9 collective-permute-start.1
  137.4 6.3 %collective-permute-done.1 = bf16[2,256,64]{1,2,0:T(8,128)(2,1)S(1)} collective-permute-done((bf16[2,256,64]{1,2,0:T(8,128)(2,1)S(1)}, bf16[2,256,64]{1,2,0:T(8,128)(2,1)S(1)}, u32[]{:S(2)}, u32[]{:S(2)}) %collective-permute-start.1) | collective-permute-done | bytes 65568 | tf_op jit(solution)/shard_map/while/body/eval_jaxpr/ppermute | solution.py:27
  144.3 0.1 constant_dynamic-update-slice_fusion.18
  144.9 2.1 fusion.91
  147.1 1.9 collective-permute-start
  149.0 3.9 collective-permute-start.1
  153.0 4.3 %collective-permute-done.1 = bf16[2,256,64]{1,2,0:T(8,128)(2,1)S(1)} collective-permute-done((bf16[2,256,64]{1,2,0:T(8,128)(2,1)S(1)}, bf16[2,256,64]{1,2,0:T(8,128)(2,1)S(1)}, u32[]{:S(2)}, u32[]{:S(2)}) %collective-permute-start.1) | collective-permute-done | bytes 65568 | tf_op jit(solution)/shard_map/while/body/eval_jaxpr/ppermute | solution.py:27
  157.9 0.1 constant_dynamic-update-slice_fusion.18
  158.5 2.1 fusion.91
  160.6 1.9 collective-permute-start
  162.6 3.9 collective-permute-start.1
  166.5 4.3 %collective-permute-done.1 = bf16[2,256,64]{1,2,0:T(8,128)(2,1)S(1)} collective-permute-done((bf16[2,256,64]{1,2,0:T(8,128)(2,1)S(1)}, bf16[2,256,64]{1,2,0:T(8,128)(2,1)S(1)}, u32[]{:S(2)}, u32[]{:S(2)}) %collective-permute-start.1) | collective-permute-done | bytes 65568 | tf_op jit(solution)/shard_map/while/body/eval_jaxpr/ppermute | solution.py:27
  171.5 0.1 constant_dynamic-update-slice_fusion.18
  172.1 2.1 fusion.91
  174.2 1.9 collective-permute-start
  176.1 3.9 collective-permute-start.1
  180.1 4.3 %collective-permute-done.1 = bf16[2,256,64]{1,2,0:T(8,128)(2,1)S(1)} collective-permute-done((bf16[2,256,64]{1,2,0:T(8,128)(2,1)S(1)}, bf16[2,256,64]{1,2,0:T(8,128)(2,1)S(1)}, u32[]{:S(2)}, u32[]{:S(2)}) %collective-permute-start.1) | collective-permute-done | bytes 65568 | tf_op jit(solution)/shard_map/while/body/eval_jaxpr/ppermute | solution.py:27
  185.0 0.1 constant_dynamic-update-slice_fusion.18
  185.6 2.1 fusion.91
  187.8 1.9 collective-permute-start
  189.7 3.9 collective-permute-start.1
  193.7 4.3 %collective-permute-done.1 = bf16[2,256,64]{1,2,0:T(8,128)(2,1)S(1)} collective-permute-done((bf16[2,256,64]{1,2,0:T(8,128)(2,1)S(1)}, bf16[2,256,64]{1,2,0:T(8,128)(2,1)S(1)}, u32[]{:S(2)}, u32[]{:S(2)}) %collective-permute-start.1) | collective-permute-done | bytes 65568 | tf_op jit(solution)/shard_map/while/body/eval_jaxpr/ppermute | solution.py:27
  198.6 0.1 constant_dynamic-update-slice_fusion.18
  199.2 2.1 fusion.91
  201.3 1.9 collective-permute-start
  203.3 3.9 collective-permute-start.1
  207.2 4.3 %collective-permute-done.1 = bf16[2,256,64]{1,2,0:T(8,128)(2,1)S(1)} collective-permute-done((bf16[2,256,64]{1,2,0:T(8,128)(2,1)S(1)}, bf16[2,256,64]{1,2,0:T(8,128)(2,1)S(1)}, u32[]{:S(2)}, u32[]{:S(2)}) %collective-permute-start.1) | collective-permute-done | bytes 65568 | tf_op jit(solution)/shard_map/while/body/eval_jaxpr/ppermute | solution.py:27
  212.2 0.1 constant_dynamic-update-slice_fusion.18
  212.8 2.1 fusion.91
  214.9 1.9 collective-permute-start
  216.8 3.9 collective-permute-start.1
  220.8 4.3 %collective-permute-done.1 = bf16[2,256,64]{1,2,0:T(8,128)(2,1)S(1)} collective-permute-done((bf16[2,256,64]{1,2,0:T(8,128)(2,1)S(1)}, bf16[2,256,64]{1,2,0:T(8,128)(2,1)S(1)}, u32[]{:S(2)}, u32[]{:S(2)}) %collective-permute-start.1) | collective-permute-done | bytes 65568 | tf_op jit(solution)/shard_map/while/body/eval_jaxpr/ppermute | solution.py:27
  226.3 2.1 fusion.91
  228.5 1.9 collective-permute-start
  230.4 3.9 collective-permute-start.1
  234.4 4.3 %collective-permute-done.1 = bf16[2,256,64]{1,2,0:T(8,128)(2,1)S(1)} collective-permute-done((bf16[2,256,64]{1,2,0:T(8,128)(2,1)S(1)}, bf16[2,256,64]{1,2,0:T(8,128)(2,1)S(1)}, u32[]{:S(2)}, u32[]{:S(2)}) %collective-permute-start.1) | collective-permute-done | bytes 65568 | tf_op jit(solution)/shard_map/while/body/eval_jaxpr/ppermute | solution.py:27
  239.9 2.1 fusion.91
  242.0 0.2 fusion.54
  242.2 0.7 fusion.58
  242.9 1.2 broadcast_in_dim.201
  244.1 5.4 %all-to-all-start.1 = ((bf16[64,2,11,256]{3,1,2,0:T(2,128)(2,1)}), bf16[64,2,11,256]{3,1,2,0:T(2,128)(2,1)S(1)}, u32[]{:S(2)}, u32[]{:S(2)}) async-start(bf16[64,2,11,256]{3,1,2,0:T(2,128)(2,1)} %broadcast_in_dim.201), calls=%async_computation.1 | async-start | bytes 1441792 | tf_op jit(solution)/shard_map/all_to_all | solution.py:41
  249.6 29.3 %all-to-all-done.1 = bf16[64,2,11,256]{3,1,2,0:T(2,128)(2,1)S(1)} async-done(((bf16[64,2,11,256]{3,1,2,0:T(2,128)(2,1)}), bf16[64,2,11,256]{3,1,2,0:T(2,128)(2,1)S(1)}, u32[]{:S(2)}, u32[]{:S(2)}) %all-to-all-start.1) | async-done | bytes 720928 | tf_op jit(solution)/shard_map/all_to_all | solution.py:41
  279.0 0.1 copy.36
  279.1 1.5 reshape.133
  280.6 6.5 %fusion.35 = f32[2,11,256]{2,1,0:T(8,128)S(1)} fusion(bf16[2,11,16384]{2,1,0:T(8,128)(2,1)} %reshape.133, s32[2,256]{1,0:T(2,128)S(1)} %copy-done.7), kind=kOutput, calls=%fused_computation.59 | convolution fusion | flops 192954880 | bytes 745472 | tf_op jit(solution)/shard_map/fkn,fnp->fkp/dot_general | solution.py:124
  287.1 0.3 fusion.30
  287.5 13.0 %all_gather.14 = bf16[2,64,1024]{2,1,0:T(8,128)(2,1)} all-gather(bf16[2,64,256]{2,1,0:T(8,128)(2,1)S(1)} %fusion.30), channel_id=1, replica_groups=mesh['phase'=8,'wide_0'=4,'wide_1'=16] {'wide_0'}, dimensions={2}, use_global_device_ids=true | all-gather | bytes 327680 | tf_op jit(solution)/shard_map/all_gather | solution.py:53
  300.5 10.2 %all-gather = s32[2,1024]{1,0:T(2,128)S(1)} all-gather(s32[2,256]{1,0:T(2,128)S(1)} %copy-done.4), channel_id=2, replica_groups=mesh['phase'=8,'wide_0'=4,'wide_1'=16] {'wide_0'}, dimensions={1}, use_global_device_ids=true | all-gather | bytes 10240 | tf_op jit(solution)/shard_map/all_gather | solution.py:53
  310.7 28.7 %all-gather.1 = s32[2,16384]{1,0:T(2,128)S(1)} all-gather(s32[2,1024]{1,0:T(2,128)S(1)} %all-gather), channel_id=3, replica_groups=mesh['phase'=8,'wide_0'=4,'wide_1'=16] {'wide_1'}, dimensions={1}, use_global_device_ids=true | all-gather | bytes 139264 | tf_op jit(solution)/shard_map/all_gather | solution.py:53
  339.5 31.0 %all-gather.4.cloned.1.call-done = bf16[2,64,16384]{2,1,0:T(8,128)(2,1)} async-done(((bf16[2,64,1024]{2,1,0:T(8,128)(2,1)}), bf16[2,64,16384]{2,1,0:T(8,128)(2,1)}) %all-gather.4.cloned.1.call-update) | async-done | bytes 4194320 | tf_op jit(solution)/shard_map/all_gather | solution.py:53
  370.5 6.7 %fusion.31 = bf16[2,128,64]{1,2,0:T(8,128)(2,1)S(1)} fusion(bf16[2,64,16384]{2,1,0:T(8,128)(2,1)} %all-gather.4.cloned.1.call-done, s32[2,16384]{1,0:T(2,128)S(1)} %broadcast_subtract_fusion), kind=kOutput, calls=%fused_computation.55 | convolution fusion | flops 541081600 | bytes 4358144 | tf_op jit(solution)/shard_map/fjp,fpc->cfj/dot_general | solution.py:139
  377.3 2.5 collective-permute-start.2
  379.8 5.5 %collective-permute-start.3 = (bf16[128,128]{0,1:T(8,128)(2,1)S(1)}, bf16[128,128]{0,1:T(8,128)(2,1)S(1)}, u32[]{:S(2)}, u32[]{:S(2)}) collective-permute-start(bf16[128,128]{0,1:T(8,128)(2,1)S(1)} %bitcast.79), channel_id=1, source_target_pairs={{1,0},{2,1},{3,2},{4,3},{5,4},{6,5},{7,6},{8,7},{9,8},{10,9},{11,1... | collective-permute-start | bytes 98312 | tf_op jit(solution)/shard_map/ppermute | solution.py:28
  385.3 1.6 collective-permute-done.3
  386.8 0.1 fusion.42
  386.9 0.2 fusion.48
  387.3 0.5 fusion.27
  387.8 0.6 copy.33
  (173 shorter events, 9.1 us)
Async XLA Ops:
  7.2 10.8 %copy-start = (bf16[16,256,256]{2,1,0:T(8,128)(2,1)S(1)}, bf16[16,256,256]{2,1,0:T(8,128)(2,1)}, u32[]{:S(2)}) copy-start(bf16[16,256,256]{2,1,0:T(8,128)(2,1)} %param.12) | copy-start | bytes 6291460
  12.8 110.9 %all-to-all-start = ((bf16[8,256,2304]{2,1,0:T(8,128)(2,1)}), bf16[8,256,2304]{2,1,0:T(8,128)(2,1)}, u32[]{:S(2)}, u32[]{:S(2)}) async-start(bf16[8,256,2304]{2,1,0:T(8,128)(2,1)} %concatenate.86), calls=%async_computation | async-start | bytes 18874368 | tf_op jit(solution)/shard_map/all_to_all | solution.py:17
  123.7 118.3 %copy-start.3 = (bf16[11,256]{1,0:T(8,128)(2,1)S(1)}, bf16[11,256]{1,0:T(8,128)(2,1)}, u32[]{:S(2)}) copy-start(bf16[11,256]{1,0:T(8,128)(2,1)} %param.14) | copy-start | bytes 16900
  123.7 20.0 %collective-permute-start = (bf16[2,256,64]{1,2,0:T(8,128)(2,1)S(1)}, bf16[2,256,64]{1,2,0:T(8,128)(2,1)S(1)}, u32[]{:S(2)}, u32[]{:S(2)}) collective-permute-start(bf16[2,256,64]{1,2,0:T(8,128)(2,1)S(1)} %get-tuple-element.195), channel_id=1, source_target_pairs={{1,0},{2,1},{3,2},{4,3},{5,4},{6,5},{7,6},{8,7},{9,8},{10,9},{11,1... | collective-permute-start | bytes 196616 | tf_op jit(solution)/shard_map/while/body/eval_jaxpr/ppermute | solution.py:28
  135.4 8.3 %collective-permute-start.1 = (bf16[2,256,64]{1,2,0:T(8,128)(2,1)S(1)}, bf16[2,256,64]{1,2,0:T(8,128)(2,1)S(1)}, u32[]{:S(2)}, u32[]{:S(2)}) collective-permute-start(bf16[2,256,64]{1,2,0:T(8,128)(2,1)S(1)} %get-tuple-element.196), channel_id=1, source_target_pairs={{0,1},{1,2},{2,3},{3,4},{4,5},{5,6},{6,7},{7,8},{8,9},{9,10},{10,1... | collective-permute-start | bytes 196616 | tf_op jit(solution)/shard_map/while/body/eval_jaxpr/ppermute | solution.py:27
  147.1 10.2 %collective-permute-start = (bf16[2,256,64]{1,2,0:T(8,128)(2,1)S(1)}, bf16[2,256,64]{1,2,0:T(8,128)(2,1)S(1)}, u32[]{:S(2)}, u32[]{:S(2)}) collective-permute-start(bf16[2,256,64]{1,2,0:T(8,128)(2,1)S(1)} %get-tuple-element.195), channel_id=1, source_target_pairs={{1,0},{2,1},{3,2},{4,3},{5,4},{6,5},{7,6},{8,7},{9,8},{10,9},{11,1... | collective-permute-start | bytes 196616 | tf_op jit(solution)/shard_map/while/body/eval_jaxpr/ppermute | solution.py:28
  149.0 8.3 %collective-permute-start.1 = (bf16[2,256,64]{1,2,0:T(8,128)(2,1)S(1)}, bf16[2,256,64]{1,2,0:T(8,128)(2,1)S(1)}, u32[]{:S(2)}, u32[]{:S(2)}) collective-permute-start(bf16[2,256,64]{1,2,0:T(8,128)(2,1)S(1)} %get-tuple-element.196), channel_id=1, source_target_pairs={{0,1},{1,2},{2,3},{3,4},{4,5},{5,6},{6,7},{7,8},{8,9},{9,10},{10,1... | collective-permute-start | bytes 196616 | tf_op jit(solution)/shard_map/while/body/eval_jaxpr/ppermute | solution.py:27
  160.6 10.2 %collective-permute-start = (bf16[2,256,64]{1,2,0:T(8,128)(2,1)S(1)}, bf16[2,256,64]{1,2,0:T(8,128)(2,1)S(1)}, u32[]{:S(2)}, u32[]{:S(2)}) collective-permute-start(bf16[2,256,64]{1,2,0:T(8,128)(2,1)S(1)} %get-tuple-element.195), channel_id=1, source_target_pairs={{1,0},{2,1},{3,2},{4,3},{5,4},{6,5},{7,6},{8,7},{9,8},{10,9},{11,1... | collective-permute-start | bytes 196616 | tf_op jit(solution)/shard_map/while/body/eval_jaxpr/ppermute | solution.py:28
  162.6 8.3 %collective-permute-start.1 = (bf16[2,256,64]{1,2,0:T(8,128)(2,1)S(1)}, bf16[2,256,64]{1,2,0:T(8,128)(2,1)S(1)}, u32[]{:S(2)}, u32[]{:S(2)}) collective-permute-start(bf16[2,256,64]{1,2,0:T(8,128)(2,1)S(1)} %get-tuple-element.196), channel_id=1, source_target_pairs={{0,1},{1,2},{2,3},{3,4},{4,5},{5,6},{6,7},{7,8},{8,9},{9,10},{10,1... | collective-permute-start | bytes 196616 | tf_op jit(solution)/shard_map/while/body/eval_jaxpr/ppermute | solution.py:27
  174.2 10.2 %collective-permute-start = (bf16[2,256,64]{1,2,0:T(8,128)(2,1)S(1)}, bf16[2,256,64]{1,2,0:T(8,128)(2,1)S(1)}, u32[]{:S(2)}, u32[]{:S(2)}) collective-permute-start(bf16[2,256,64]{1,2,0:T(8,128)(2,1)S(1)} %get-tuple-element.195), channel_id=1, source_target_pairs={{1,0},{2,1},{3,2},{4,3},{5,4},{6,5},{7,6},{8,7},{9,8},{10,9},{11,1... | collective-permute-start | bytes 196616 | tf_op jit(solution)/shard_map/while/body/eval_jaxpr/ppermute | solution.py:28
  176.1 8.3 %collective-permute-start.1 = (bf16[2,256,64]{1,2,0:T(8,128)(2,1)S(1)}, bf16[2,256,64]{1,2,0:T(8,128)(2,1)S(1)}, u32[]{:S(2)}, u32[]{:S(2)}) collective-permute-start(bf16[2,256,64]{1,2,0:T(8,128)(2,1)S(1)} %get-tuple-element.196), channel_id=1, source_target_pairs={{0,1},{1,2},{2,3},{3,4},{4,5},{5,6},{6,7},{7,8},{8,9},{9,10},{10,1... | collective-permute-start | bytes 196616 | tf_op jit(solution)/shard_map/while/body/eval_jaxpr/ppermute | solution.py:27
  187.8 10.2 %collective-permute-start = (bf16[2,256,64]{1,2,0:T(8,128)(2,1)S(1)}, bf16[2,256,64]{1,2,0:T(8,128)(2,1)S(1)}, u32[]{:S(2)}, u32[]{:S(2)}) collective-permute-start(bf16[2,256,64]{1,2,0:T(8,128)(2,1)S(1)} %get-tuple-element.195), channel_id=1, source_target_pairs={{1,0},{2,1},{3,2},{4,3},{5,4},{6,5},{7,6},{8,7},{9,8},{10,9},{11,1... | collective-permute-start | bytes 196616 | tf_op jit(solution)/shard_map/while/body/eval_jaxpr/ppermute | solution.py:28
  189.7 8.3 %collective-permute-start.1 = (bf16[2,256,64]{1,2,0:T(8,128)(2,1)S(1)}, bf16[2,256,64]{1,2,0:T(8,128)(2,1)S(1)}, u32[]{:S(2)}, u32[]{:S(2)}) collective-permute-start(bf16[2,256,64]{1,2,0:T(8,128)(2,1)S(1)} %get-tuple-element.196), channel_id=1, source_target_pairs={{0,1},{1,2},{2,3},{3,4},{4,5},{5,6},{6,7},{7,8},{8,9},{9,10},{10,1... | collective-permute-start | bytes 196616 | tf_op jit(solution)/shard_map/while/body/eval_jaxpr/ppermute | solution.py:27
  201.3 10.2 %collective-permute-start = (bf16[2,256,64]{1,2,0:T(8,128)(2,1)S(1)}, bf16[2,256,64]{1,2,0:T(8,128)(2,1)S(1)}, u32[]{:S(2)}, u32[]{:S(2)}) collective-permute-start(bf16[2,256,64]{1,2,0:T(8,128)(2,1)S(1)} %get-tuple-element.195), channel_id=1, source_target_pairs={{1,0},{2,1},{3,2},{4,3},{5,4},{6,5},{7,6},{8,7},{9,8},{10,9},{11,1... | collective-permute-start | bytes 196616 | tf_op jit(solution)/shard_map/while/body/eval_jaxpr/ppermute | solution.py:28
  203.3 8.3 %collective-permute-start.1 = (bf16[2,256,64]{1,2,0:T(8,128)(2,1)S(1)}, bf16[2,256,64]{1,2,0:T(8,128)(2,1)S(1)}, u32[]{:S(2)}, u32[]{:S(2)}) collective-permute-start(bf16[2,256,64]{1,2,0:T(8,128)(2,1)S(1)} %get-tuple-element.196), channel_id=1, source_target_pairs={{0,1},{1,2},{2,3},{3,4},{4,5},{5,6},{6,7},{7,8},{8,9},{9,10},{10,1... | collective-permute-start | bytes 196616 | tf_op jit(solution)/shard_map/while/body/eval_jaxpr/ppermute | solution.py:27
  214.9 10.2 %collective-permute-start = (bf16[2,256,64]{1,2,0:T(8,128)(2,1)S(1)}, bf16[2,256,64]{1,2,0:T(8,128)(2,1)S(1)}, u32[]{:S(2)}, u32[]{:S(2)}) collective-permute-start(bf16[2,256,64]{1,2,0:T(8,128)(2,1)S(1)} %get-tuple-element.195), channel_id=1, source_target_pairs={{1,0},{2,1},{3,2},{4,3},{5,4},{6,5},{7,6},{8,7},{9,8},{10,9},{11,1... | collective-permute-start | bytes 196616 | tf_op jit(solution)/shard_map/while/body/eval_jaxpr/ppermute | solution.py:28
  216.8 8.3 %collective-permute-start.1 = (bf16[2,256,64]{1,2,0:T(8,128)(2,1)S(1)}, bf16[2,256,64]{1,2,0:T(8,128)(2,1)S(1)}, u32[]{:S(2)}, u32[]{:S(2)}) collective-permute-start(bf16[2,256,64]{1,2,0:T(8,128)(2,1)S(1)} %get-tuple-element.196), channel_id=1, source_target_pairs={{0,1},{1,2},{2,3},{3,4},{4,5},{5,6},{6,7},{7,8},{8,9},{9,10},{10,1... | collective-permute-start | bytes 196616 | tf_op jit(solution)/shard_map/while/body/eval_jaxpr/ppermute | solution.py:27
  228.5 10.2 %collective-permute-start = (bf16[2,256,64]{1,2,0:T(8,128)(2,1)S(1)}, bf16[2,256,64]{1,2,0:T(8,128)(2,1)S(1)}, u32[]{:S(2)}, u32[]{:S(2)}) collective-permute-start(bf16[2,256,64]{1,2,0:T(8,128)(2,1)S(1)} %get-tuple-element.195), channel_id=1, source_target_pairs={{1,0},{2,1},{3,2},{4,3},{5,4},{6,5},{7,6},{8,7},{9,8},{10,9},{11,1... | collective-permute-start | bytes 196616 | tf_op jit(solution)/shard_map/while/body/eval_jaxpr/ppermute | solution.py:28
  230.4 8.3 %collective-permute-start.1 = (bf16[2,256,64]{1,2,0:T(8,128)(2,1)S(1)}, bf16[2,256,64]{1,2,0:T(8,128)(2,1)S(1)}, u32[]{:S(2)}, u32[]{:S(2)}) collective-permute-start(bf16[2,256,64]{1,2,0:T(8,128)(2,1)S(1)} %get-tuple-element.196), channel_id=1, source_target_pairs={{0,1},{1,2},{2,3},{3,4},{4,5},{5,6},{6,7},{7,8},{8,9},{9,10},{10,1... | collective-permute-start | bytes 196616 | tf_op jit(solution)/shard_map/while/body/eval_jaxpr/ppermute | solution.py:27
  242.0 7.5 %copy-start.8 = (s32[2,1]{0,1:T(1,128)S(1)}, s32[2,1]{0,1:T(1,128)}, u32[]{:S(2)}) copy-start(s32[2,1]{0,1:T(1,128)} %param.18) | copy-start | bytes 28
  244.1 36.5 %copy-start.7 = (s32[2,256]{1,0:T(2,128)S(1)}, s32[2,256]{1,0:T(2,128)}, u32[]{:S(2)}) copy-start(s32[2,256]{1,0:T(2,128)} %param.16) | copy-start | bytes 6148
  244.1 34.9 %all-to-all-start.1 = ((bf16[64,2,11,256]{3,1,2,0:T(2,128)(2,1)}), bf16[64,2,11,256]{3,1,2,0:T(2,128)(2,1)S(1)}, u32[]{:S(2)}, u32[]{:S(2)}) async-start(bf16[64,2,11,256]{3,1,2,0:T(2,128)(2,1)} %broadcast_in_dim.201), calls=%async_computation.1 | async-start | bytes 1441792 | tf_op jit(solution)/shard_map/all_to_all | solution.py:41
  249.5 121.0 %all-gather.4.cloned.1.call-start = ((), (), s32[]{:S(2)}) async-start(), calls=%async_computation.2 | async-start | bytes 4456448 | tf_op jit(solution)/shard_map/all_gather | solution.py:53
  280.6 6.6 %copy-start.5 = (f32[2,4,256]{2,1,0:T(4,128)S(1)}, f32[2,4,256]{2,1,0:T(4,128)}, u32[]{:S(2)}) copy-start(f32[2,4,256]{2,1,0:T(4,128)} %param.15) | copy-start | bytes 24580
  280.6 6.6 %copy-start.6 = (f32[64,15]{0,1:T(8,128)S(1)}, f32[64,15]{0,1:T(8,128)}, u32[]{:S(2)}) copy-start(f32[64,15]{0,1:T(8,128)} %param.19) | copy-start | bytes 11524
  280.6 19.9 %copy-start.4 = (s32[2,256]{1,0:T(2,128)S(1)}, s32[2,256]{1,0:T(2,128)}, u32[]{:S(2)}) copy-start(s32[2,256]{1,0:T(2,128)} %param.17) | copy-start | bytes 6148
  339.5 47.8 %copy-start.1 = (bf16[576,384]{1,0:T(8,128)(2,1)S(1)}, bf16[576,384]{1,0:T(8,128)(2,1)}, u32[]{:S(2)}) copy-start(bf16[576,384]{1,0:T(8,128)(2,1)} %param.20) | copy-start | bytes 1327108
  339.5 47.8 %copy-start.2 = (bf16[384,20]{0,1:T(8,128)(2,1)S(1)}, bf16[384,20]{0,1:T(8,128)(2,1)}, u32[]{:S(2)}) copy-start(bf16[384,20]{0,1:T(8,128)(2,1)} %param.21) | copy-start | bytes 46084
  377.3 8.0 %collective-permute-start.2 = (bf16[128,128]{0,1:T(8,128)(2,1)S(1)}, bf16[128,128]{0,1:T(8,128)(2,1)S(1)}, u32[]{:S(2)}, u32[]{:S(2)}) collective-permute-start(bf16[128,128]{0,1:T(8,128)(2,1)S(1)} %bitcast.78), channel_id=1, source_target_pairs={{0,1},{1,2},{2,3},{3,4},{4,5},{5,6},{6,7},{7,8},{8,9},{9,10},{10,1... | collective-permute-start | bytes 98312 | tf_op jit(solution)/shard_map/ppermute | solution.py:27
  379.8 7.0 %collective-permute-start.3 = (bf16[128,128]{0,1:T(8,128)(2,1)S(1)}, bf16[128,128]{0,1:T(8,128)(2,1)S(1)}, u32[]{:S(2)}, u32[]{:S(2)}) collective-permute-start(bf16[128,128]{0,1:T(8,128)(2,1)S(1)} %bitcast.79), channel_id=1, source_target_pairs={{1,0},{2,1},{3,2},{4,3},{5,4},{6,5},{7,6},{8,7},{9,8},{10,9},{11,1... | collective-permute-start | bytes 98312 | tf_op jit(solution)/shard_map/ppermute | solution.py:28
Sparse Core Ops, SparseCore 0:
  300.6 69.8 all-gather.3
